TPU v7x, 32 devices: a whole 2x2x4 slice. The times are simulated.
32 devices in a mesh: pop: 16 (over z, x, core), hid: 2 (over y).
Axes of the slice: x: 2, y: 2, z: 4, core: 2. Of those that a mesh axis runs over, the one named last changes fastest.
Arguments:
- tokens: bfloat16 [512, 4096], P('pop', 'hid'), may hold values from -6 to 6
- fitness_ranks: int32 [32], replicated, may hold values from 0 to 31, each once
- gate_weight: bfloat16 [4096, 16384], P('hid', 'pop'), may hold values from -0.09375 to 0.09375
- up_weight: bfloat16 [4096, 16384], P('hid', 'pop'), may hold values from -0.09375 to 0.09375
- down_weight: bfloat16 [16384, 4096], P('pop', 'hid'), may hold values from -0.046875 to 0.046875
- gate_input_factor: bfloat16 [32, 4, 4096], P(None, None, 'hid'), may hold values from -6 to 6
- up_input_factor: bfloat16 [32, 4, 4096], P(None, None, 'hid'), may hold values from -6 to 6
- down_right: bfloat16 [32, 4, 4096], P(None, None, 'hid'), may hold values from -6 to 6
- gate_output_factor: bfloat16 [32, 4, 16384], P('pop'), may hold values from -6 to 6
- up_output_factor: bfloat16 [32, 4, 16384], P('pop'), may hold values from -6 to 6
- down_left: bfloat16 [32, 4, 16384], P('pop'), may hold values from -6 to 6
Outputs:
- mixed: bfloat16 [512, 4096], P('pop', 'hid')
- gate_step: float32 [4096, 16384], P('hid', 'pop')
- up_step: float32 [4096, 16384], P('hid', 'pop')
- down_step: float32 [16384, 4096], P('pop', 'hid')
Inputs may be any that keep to these rules, and one draw needn't show every extreme that they name: `fitness_ranks`: every rank appears exactly once.
All inputs are finite; a program needn't handle non-finite values.
Results may differ from a plain program's by a relative error of at most 0.025.
Values may be sent and summed in bfloat16 or wider, within the bound.
No kernel may reach another device: no remote copies, remote signals or barrier semaphores. Data moves between devices by JAX's collectives and lax.ppermute only.
A program may use at most 128 MiB of HBM per device.

v0:
```python
import math
import jax
import jax.numpy as jnp
from jax import lax
from jax.sharding import PartitionSpec as P

MODEL_WIDTH = 4096
HIDDEN_UNITS = 16384
RANK = 4
SAMPLE_LENGTH = 16


def local(
    tokens,
    fitness_ranks,
    gate_weight,
    up_weight,
    down_weight,
    gate_input_factor,
    up_input_factor,
    down_right,
    gate_output_factor,
    up_output_factor,
    down_left,
):
    scalar_real = jnp.float32
    pop_count = lax.axis_size("pop")
    hid_count = lax.axis_size("hid")
    pop_index = lax.axis_index("pop")
    hid_index = lax.axis_index("hid")
    tok_local = tokens.shape[0]
    mem_local = tok_local // SAMPLE_LENGTH
    members = mem_local * pop_count
    total_rows = tok_local * pop_count
    row_block_count = total_rows // hid_count
    block_members = row_block_count // SAMPLE_LENGTH
    width_part = tokens.shape[1]
    hidden_portion = gate_weight.shape[1]
    scale_in = 0.5 / math.sqrt(MODEL_WIDTH * RANK)
    scale_out = 0.5 / math.sqrt(HIDDEN_UNITS * RANK)
    fitness = fitness_ranks.astype(scalar_real) / (members - 1) - 0.5
    member_token_rows = tokens.reshape(mem_local, SAMPLE_LENGTH, width_part)
    member_gate_input = lax.dynamic_slice_in_dim(
        gate_input_factor, pop_index * mem_local, mem_local, 0
    )
    member_up_input = lax.dynamic_slice_in_dim(up_input_factor, pop_index * mem_local, mem_local, 0)
    gate_projection = jnp.einsum(
        "otl,ozl->otz", member_token_rows, member_gate_input, preferred_element_type=scalar_real
    )
    up_projection = jnp.einsum(
        "otl,ozl->otz", member_token_rows, member_up_input, preferred_element_type=scalar_real
    )
    gate_projection, up_projection = lax.psum((gate_projection, up_projection), "hid")
    gate_projection, up_projection = (
        lax.all_gather(gate_projection, "pop", axis=0, tiled=True),
        lax.all_gather(up_projection, "pop", axis=0, tiled=True),
    )
    gate_cols, up_cols, down_cols = (
        lax.all_to_all(gate_output_factor, "pop", split_axis=2, concat_axis=0, tiled=True),
        lax.all_to_all(up_output_factor, "pop", split_axis=2, concat_axis=0, tiled=True),
        lax.all_to_all(down_left, "pop", split_axis=2, concat_axis=0, tiled=True),
    )
    gathered = lax.all_gather(tokens, "pop", axis=0, tiled=True)
    paired = jnp.concatenate([gate_weight, up_weight], axis=1)
    picked = gathered
    sums = lax.psum_scatter(
        jnp.dot(picked, paired, preferred_element_type=scalar_real).astype(jnp.bfloat16),
        "hid",
        scatter_dimension=0,
        tiled=True,
    ).astype(jnp.float32)
    gate_sum = sums[:, :hidden_portion]
    up_sum = sums[:, hidden_portion:]
    first_member = hid_index * block_members
    gate_tile_block = lax.dynamic_slice_in_dim(gate_projection, first_member, block_members, 0)
    up_tile_block = lax.dynamic_slice_in_dim(up_projection, first_member, block_members, 0)
    gate_vectors = lax.dynamic_slice_in_dim(gate_cols, first_member, block_members, 0).astype(
        scalar_real
    )
    up_vectors = lax.dynamic_slice_in_dim(up_cols, first_member, block_members, 0).astype(
        scalar_real
    )
    gate_lowrank_term = jnp.einsum("iln,ina->ila", gate_tile_block, gate_vectors).reshape(
        row_block_count, hidden_portion
    )
    up_lowrank_term = jnp.einsum("iln,ina->ila", up_tile_block, up_vectors).reshape(
        row_block_count, hidden_portion
    )
    gate = gate_sum + scale_in * gate_lowrank_term
    up = up_sum + scale_in * up_lowrank_term
    hidden = (jax.nn.silu(gate) * up).astype(jnp.bfloat16)
    every_hidden = lax.all_gather(hidden, "hid", axis=0, tiled=True)
    picked = every_hidden
    member_count = lax.axis_size("pop") * tok_local // SAMPLE_LENGTH
    output_factor_portion = down_right.astype(scalar_real)
    contracting_matrix = jnp.einsum(
        "reu,ryu->rey",
        picked.reshape(member_count, SAMPLE_LENGTH, hidden_portion),
        down_cols,
        preferred_element_type=scalar_real,
    )
    lowrank_product = jnp.einsum("okw,owt->okt", contracting_matrix, output_factor_portion).reshape(
        lax.axis_size("pop") * tok_local, width_part
    )
    mixed = lax.psum_scatter(
        (
            jnp.dot(picked, down_weight, preferred_element_type=scalar_real)
            + scale_out * lowrank_product
        ).astype(jnp.bfloat16),
        "pop",
        scatter_dimension=0,
        tiled=True,
    )
    factor = 1.0 / math.sqrt(members * RANK)
    weights3 = fitness[:, None, None]
    scaled_gate = (
        (gate_input_factor.astype(scalar_real) * weights3)
        .astype(jnp.bfloat16)
        .reshape(members * RANK, width_part)
    )
    scaled_up = (
        (up_input_factor.astype(scalar_real) * weights3)
        .astype(jnp.bfloat16)
        .reshape(members * RANK, width_part)
    )
    scaled_down = (
        (down_right.astype(scalar_real) * weights3)
        .astype(jnp.bfloat16)
        .reshape(members * RANK, width_part)
    )
    dims = (((0,), (0,)), ((), ()))
    gate_step = factor * lax.dot_general(
        scaled_gate,
        gate_cols.reshape(members * RANK, hidden_portion),
        dims,
        preferred_element_type=scalar_real,
    )
    up_step = factor * lax.dot_general(
        scaled_up,
        up_cols.reshape(members * RANK, hidden_portion),
        dims,
        preferred_element_type=scalar_real,
    )
    down_step = factor * lax.dot_general(
        down_cols.reshape(members * RANK, hidden_portion),
        scaled_down,
        dims,
        preferred_element_type=scalar_real,
    )
    return (mixed, gate_step, up_step, down_step)


def solution(mesh):
    in_specs = (
        P("pop", "hid"),
        P(),
        P("hid", "pop"),
        P("hid", "pop"),
        P("pop", "hid"),
        P(None, None, "hid"),
        P(None, None, "hid"),
        P(None, None, "hid"),
        P("pop", None, None),
        P("pop", None, None),
        P("pop", None, None),
    )
    out_specs = (P("pop", "hid"), P("hid", "pop"), P("hid", "pop"), P("pop", "hid"))
    return jax.shard_map(local, mesh=mesh, in_specs=in_specs, out_specs=out_specs, check_vma=False)
```

profile of v0, /device:TPU:0, one launch (start us, length us, event | category | flops | bytes accessed | tf_op | source)
XLA Modules:
  0.0 419.8 jit_solution(13870929993239631916)
XLA Ops:
  8.0 46.4 %all-gather.3.cloned.1.call-done = bf16[512,2048]{1,0:T(8,128)(2,1)} async-done(((bf16[32,2048]{1,0:T(8,128)(2,1)}), bf16[512,2048]{1,0:T(8,128)(2,1)}) %all-gather.3.cloned.1.call-update) | async-done | bytes 2097168 | tf_op jit(solution)/shard_map/all_gather | solution.py:63
  54.3 10.0 %fusion.8 = bf16[512,2048]{0,1:T(8,128)(2,1)} fusion(bf16[512,2048]{1,0:T(8,128)(2,1)} %all-gather.3.cloned.1.call-done, bf16[2048,1024]{1,0:T(8,128)(2,1)} %param.14, bf16[2048,1024]{1,0:T(8,128)(2,1)} %param.13), kind=kOutput, calls=%fused_computation.11 | convolution fusion | flops 4312793088 | bytes 12582912 | tf_op jit(solution)/shard_map/dot_general | solution.py:67
  64.3 13.0 %copy.27 = bf16[2,4,16384]{1,0,2:T(2,128)(2,1)} copy(bf16[2,4,16384]{2,1,0:T(4,128)(2,1)S(1)} %copy-done.5) | data formatting | bytes 524288 | tf_op args[8]
  77.3 16.9 %reshape.55 = bf16[16,2,4096]{2,1,0:T(2,128)(2,1)} reshape(bf16[16384,2,4]{2,1,0:T(2,128)(2,1)} %bitcast.51) | data formatting | bytes 524288
  94.2 3.5 all-to-all-start
  97.7 13.0 %copy.30 = bf16[2,4,16384]{1,0,2:T(2,128)(2,1)} copy(bf16[2,4,16384]{2,1,0:T(4,128)(2,1)S(1)} %copy-done.6) | data formatting | bytes 524288 | tf_op args[9]
  110.7 16.9 %reshape.53 = bf16[16,2,4096]{2,1,0:T(2,128)(2,1)} reshape(bf16[16384,2,4]{2,1,0:T(2,128)(2,1)} %bitcast.52) | data formatting | bytes 524288
  127.5 6.0 %all-to-all-start.1 = ((bf16[16,2,4096]{2,1,0:T(2,128)(2,1)}), bf16[16,2,4096]{2,1,0:T(2,128)(2,1)S(1)}, u32[]{:S(2)}, u32[]{:S(2)}) async-start(bf16[16,2,4096]{2,1,0:T(2,128)(2,1)} %reshape.53), calls=%async_computation.2 | async-start | bytes 524288 | tf_op jit(solution)/shard_map/all_to_all | solution.py:60
  134.5 0.9 convolution_bitcast_fusion.1
  135.4 5.0 %all-reduce = (bf16[2,16,4]{1,2,0:T(4,128)(2,1)S(1)}, bf16[2,16,4]{1,2,0:T(4,128)(2,1)S(1)}) all-reduce(f32[2,16,4]{1,2,0:T(4,128)S(1)} %convolution_bitcast_fusion, f32[2,16,4]{1,2,0:T(4,128)S(1)} %convolution_bitcast_fusion.1), channel_id=1, replica_groups=mesh['pop'=16,'hid'=2] {'hid'}, use_global_device_ids=true, to_apply=%region_2.0 | all-reduce | flops 256 | bytes 1536 | tf_op jit(solution)/shard_map/psum | solution.py:53
  140.4 21.8 %all_gather.13 = bf16[32,16,4]{1,2,0:T(4,128)(2,1)S(1)} all-gather(bf16[2,16,4]{1,2,0:T(4,128)(2,1)S(1)} %get-tuple-element.17), channel_id=1, replica_groups=mesh['pop'=16,'hid'=2] {'pop'}, dimensions={0}, use_global_device_ids=true | all-gather | bytes 4352 | tf_op jit(solution)/shard_map/all_gather | solution.py:55
  162.2 17.7 %all_gather.14 = bf16[32,16,4]{1,2,0:T(4,128)(2,1)S(1)} all-gather(bf16[2,16,4]{1,2,0:T(4,128)(2,1)S(1)} %get-tuple-element.16), channel_id=1, replica_groups=mesh['pop'=16,'hid'=2] {'pop'}, dimensions={0}, use_global_device_ids=true | all-gather | bytes 4352 | tf_op jit(solution)/shard_map/all_gather | solution.py:56
  179.8 19.0 %reshape.56 = bf16[16384,2,4]{2,1,0:T(2,128)(2,1)} reshape(bf16[16,2,4096]{2,1,0:T(2,128)(2,1)S(1)} %all-to-all-done) | data formatting | bytes 524288
  198.9 19.2 %copy.28 = bf16[2,4,16,1024]{3,1,0,2:T(4,128)(2,1)S(1)} copy(bf16[2,4,16,1024]{1,0,3,2:T(2,128)(2,1)} %bitcast.48) | data formatting | bytes 524288 | tf_op jit(solution)/shard_map/all_to_all | solution.py:59
  218.8 19.1 %reshape.54 = bf16[16384,2,4]{2,1,0:T(2,128)(2,1)} reshape(bf16[16,2,4096]{2,1,0:T(2,128)(2,1)S(1)} %all-to-all-done.1) | data formatting | bytes 524288
  237.8 19.2 %copy.31 = bf16[2,4,16,1024]{3,1,0,2:T(4,128)(2,1)S(1)} copy(bf16[2,4,16,1024]{1,0,3,2:T(2,128)(2,1)} %bitcast.49) | data formatting | bytes 524288 | tf_op jit(solution)/shard_map/all_to_all | solution.py:60
  258.1 1.4 convert_element_type.41
  259.5 1.2 fusion.14
  260.8 13.0 %copy.34 = bf16[2,4,16384]{1,0,2:T(2,128)(2,1)} copy(bf16[2,4,16384]{2,1,0:T(4,128)(2,1)S(1)} %copy-done.7) | data formatting | bytes 524288 | tf_op args[10]
  273.8 16.2 %reshape.57 = bf16[16,2,4096]{2,1,0:T(2,128)(2,1)S(1)} reshape(bf16[16384,2,4]{2,1,0:T(2,128)(2,1)} %bitcast.53) | data formatting | bytes 524288
  290.0 12.9 %all_to_all.54 = bf16[16,2,4096]{2,1,0:T(2,128)(2,1)S(1)} all-to-all(bf16[16,2,4096]{2,1,0:T(2,128)(2,1)S(1)} %reshape.57), channel_id=1, replica_groups=mesh['pop'=16,'hid'=2] {'pop'}, dimensions={0} | all-to-all | bytes 524288 | tf_op jit(solution)/shard_map/all_to_all | solution.py:61
  302.9 19.0 %reshape.58 = bf16[16384,2,4]{2,1,0:T(2,128)(2,1)} reshape(bf16[16,2,4096]{2,1,0:T(2,128)(2,1)S(1)} %all_to_all.54) | data formatting | bytes 524288
  321.9 19.2 %copy.35 = bf16[2,4,16,1024]{3,1,0,2:T(4,128)(2,1)S(1)} copy(bf16[2,4,16,1024]{1,0,3,2:T(2,128)(2,1)} %bitcast.50) | data formatting | bytes 524288 | tf_op jit(solution)/shard_map/all_to_all | solution.py:61
  341.2 1.6 copy.33
  342.8 3.1 convolution_multiply_fusion.2
  345.9 7.2 %fusion.4 = bf16[512,2048]{1,0:T(8,128)(2,1)} fusion(f32[32,16,2048]{2,1,0:T(8,128)} %convolution_multiply_fusion.2, bf16[512,1024]{0,1:T(8,128)(2,1)S(1)} %copy-done, bf16[1024,2048]{1,0:T(8,128)(2,1)} %param.15), kind=kOutput, calls=%fused_computation.8 | convolution fusion | flops 2149580800 | bytes 11534336 | tf_op jit(solution)/shard_map/dot_general | solution.py:107
  353.1 2.3 multiply_convert_fusion
  355.8 4.7 %multiply_bitcast_fusion = f32[1024,2048]{0,1:T(8,128)} fusion(bf16[128,2048]{1,0:T(8,128)(2,1)S(1)} %reshape.51, bf16[128,1024]{1,0:T(8,128)(2,1)S(1)} %reshape.52), kind=kOutput, calls=%fused_computation.4 | convolution fusion | flops 538968064 | bytes 9175040 | tf_op jit(solution)/shard_map/dot_general | solution.py:144
  360.5 9.3 %copy.36 = f32[1024,2048]{1,0:T(8,128)} copy(f32[1024,2048]{0,1:T(8,128)} %multiply_bitcast_fusion) | data formatting | bytes 16777216
  370.0 4.7 %convolution_multiply_fusion = f32[2048,1024]{1,0:T(8,128)} fusion(bf16[128,2048]{1,0:T(8,128)(2,1)S(1)} %reshape.49, bf16[128,1024]{1,0:T(8,128)(2,1)S(1)} %reshape.50), kind=kOutput, calls=%fused_computation.5 | convolution fusion | flops 538968064 | bytes 9175040 | tf_op jit(solution)/shard_map/dot_general | solution.py:138
  374.6 4.7 %convolution_multiply_fusion.1 = f32[2048,1024]{1,0:T(8,128)} fusion(bf16[128,2048]{1,0:T(8,128)(2,1)S(1)} %reshape.47, bf16[128,1024]{1,0:T(8,128)(2,1)S(1)} %reshape.48), kind=kOutput, calls=%fused_computation.6 | convolution fusion | flops 538968064 | bytes 9175040 | tf_op jit(solution)/shard_map/dot_general | solution.py:132
  379.3 33.9 %reduce-scatter.5.cloned.1.call-done = bf16[32,2048]{1,0:T(8,128)(2,1)} async-done(((bf16[512,2048]{1,0:T(8,128)(2,1)}), bf16[32,2048]{1,0:T(8,128)(2,1)}) %reduce-scatter.5.cloned.1.call-update) | async-done | bytes 131088 | tf_op jit(solution)/shard_map/reduce_scatter | solution.py:105
  (42 shorter events, 4.2 us)
Async XLA Ops:
  7.2 47.2 %all-gather.3.cloned.1.call-start = ((), (), s32[]{:S(2)}) async-start(), calls=%async_computation.5 | async-start | bytes 2228224 | tf_op jit(solution)/shard_map/all_gather | solution.py:63
  7.9 56.4 %copy-start.5 = (bf16[2,4,16384]{2,1,0:T(4,128)(2,1)S(1)}, bf16[2,4,16384]{2,1,0:T(4,128)(2,1)}, u32[]{:S(2)}) copy-start(bf16[2,4,16384]{2,1,0:T(4,128)(2,1)} %param.19) | copy-start | bytes 786436
  7.9 250.2 %reduce-scatter.3.cloned.1.call-start = ((), (), s32[]{:S(2)}) async-start(), calls=%async_computation.6 | async-start | bytes 3145728 | tf_op jit(solution)/shard_map/reduce_scatter | solution.py:66
  77.3 20.4 %copy-start.6 = (bf16[2,4,16384]{2,1,0:T(4,128)(2,1)S(1)}, bf16[2,4,16384]{2,1,0:T(4,128)(2,1)}, u32[]{:S(2)}) copy-start(bf16[2,4,16384]{2,1,0:T(4,128)(2,1)} %param.20) | copy-start | bytes 786436
  94.2 33.4 %all-to-all-start = ((bf16[16,2,4096]{2,1,0:T(2,128)(2,1)}), bf16[16,2,4096]{2,1,0:T(2,128)(2,1)S(1)}, u32[]{:S(2)}, u32[]{:S(2)}) async-start(bf16[16,2,4096]{2,1,0:T(2,128)(2,1)} %reshape.55), calls=%async_computation.1 | async-start | bytes 524288 | tf_op jit(solution)/shard_map/all_to_all | solution.py:59
  110.7 22.9 %copy-start.4 = (bf16[32,2048]{1,0:T(8,128)(2,1)S(1)}, bf16[32,2048]{1,0:T(8,128)(2,1)}, u32[]{:S(2)}) copy-start(bf16[32,2048]{1,0:T(8,128)(2,1)} %param.11) | copy-start | bytes 393220
  127.5 91.2 %all-to-all-start.1 = ((bf16[16,2,4096]{2,1,0:T(2,128)(2,1)}), bf16[16,2,4096]{2,1,0:T(2,128)(2,1)S(1)}, u32[]{:S(2)}, u32[]{:S(2)}) async-start(bf16[16,2,4096]{2,1,0:T(2,128)(2,1)} %reshape.53), calls=%async_computation.2 | async-start | bytes 524288 | tf_op jit(solution)/shard_map/all_to_all | solution.py:60
  133.5 207.7 %all-gather.5.cloned.1.call-start = ((), (), s32[]{:S(2)}) async-start(), calls=%async_computation.7 | async-start | bytes 1572864 | tf_op jit(solution)/shard_map/all_gather | solution.py:92
  257.0 0.7 copy-start.2
  258.1 2.8 copy-start.7
  260.8 152.5 %reduce-scatter.5.cloned.1.call-start = ((), (), s32[]{:S(2)}) async-start(), calls=%async_computation.8 | async-start | bytes 2228224 | tf_op jit(solution)/shard_map/reduce_scatter | solution.py:105
  321.9 20.9 %copy-start.1 = (bf16[32,4,2048]{2,1,0:T(4,128)(2,1)S(1)}, bf16[32,4,2048]{2,1,0:T(4,128)(2,1)}, u32[]{:S(2)}) copy-start(bf16[32,4,2048]{2,1,0:T(4,128)(2,1)} %param.18) | copy-start | bytes 1572868
  341.2 4.7 %copy-start = (bf16[512,1024]{0,1:T(8,128)(2,1)S(1)}, bf16[512,1024]{0,1:T(8,128)(2,1)}, u32[]{:S(2)}) copy-start(bf16[512,1024]{0,1:T(8,128)(2,1)} %all-gather.5.cloned.1.call-done) | copy-start | bytes 3145732
  345.9 7.2 %copy-start.8 = (s32[32]{0:T(128)S(1)}, s32[32]{0:T(128)}, u32[]{:S(2)}) copy-start(s32[32]{0:T(128)} %param.12) | copy-start | bytes 388
  360.5 9.3 %copy-start.3 = (bf16[2,4,16,1024]{3,1,0,2:T(4,128)(2,1)S(1)}, bf16[2,4,16,1024]{3,1,0,2:T(4,128)(2,1)}, u32[]{:S(2)}) copy-start(bf16[2,4,16,1024]{3,1,0,2:T(4,128)(2,1)} %copy-done.2) | copy-start | bytes 786436
Sparse Core Ops, SparseCore 0:
  10.1 44.1 all-gather.2
  64.5 30.6 reduce-scatter.2
  260.9 19.5 all-gather.4
  353.2 59.9 reduce-scatter.4
where the time goes:
time: 422 us; the launch traced here: 420 us
  local copies, waits for them, and re-layouts  216 us (51%)
  waiting for transfers between devices  81.1 us (19%)
  blocking collectives  57.3 us (14%)
  matrix products  36.8 us (9%)
  between operations  14 us (3%)
  starting transfers between devices  9.65 us (2%)
  other arithmetic  4.9 us (1%)
    unnamed x28, local copies, waits for them, and re-layouts  156 us
    all_gather x1, waiting for transfers between devices, local(): gathered = lax.all_gather(tokens, 'pop', axis=0, tiled=True)  46.4 us
    reduce_scatter x1, waiting for transfers between devices, local(): lax.psum_scatter((jnp.dot(picked, down_weight, preferred_element_type=sca...  33.9 us
    all_gather x1, blocking collectives, local(): lax.all_gather(gate_projection, 'pop', axis=0, tiled=True)  21.8 us
    all_to_all x1, local copies, waits for them, and re-layouts, local(): lax.all_to_all(down_left, 'pop', split_axis=2, concat_axis=0, tiled=True)  19.2 us
    all_to_all x1, local copies, waits for them, and re-layouts, local(): lax.all_to_all(gate_output_factor, 'pop', split_axis=2, concat_axis=0, ti...  19.2 us
    all_to_all x1, local copies, waits for them, and re-layouts, local(): lax.all_to_all(up_output_factor, 'pop', split_axis=2, concat_axis=0, tile...  19.2 us
    all_gather x1, blocking collectives, local(): lax.all_gather(up_projection, 'pop', axis=0, tiled=True)  17.7 us
  transfers between devices with their start and end apart: 6, of which 2 were waited for; matrix products, arithmetic and copies ran while one was open for 55% of the time, Pallas kernels for 0%

commit v1 on v0

--- a/solution.py
+++ b/solution.py
@@ -58,7 +58,12 @@
     gate_cols, up_cols, down_cols = (
         lax.all_to_all(gate_output_factor, "pop", split_axis=2, concat_axis=0, tiled=True),
         lax.all_to_all(up_output_factor, "pop", split_axis=2, concat_axis=0, tiled=True),
-        lax.all_to_all(down_left, "pop", split_axis=2, concat_axis=0, tiled=True),
+        jnp.concatenate(
+            lax.all_to_all(
+                jnp.stack(jnp.split(down_left, lax.axis_size("pop"), axis=2)), "pop", 0, 0
+            ),
+            axis=0,
+        ),
     )
     gathered = lax.all_gather(tokens, "pop", axis=0, tiled=True)
     paired = jnp.concatenate([gate_weight, up_weight], axis=1)

time: 422 us -> 372 us (0.88)
  local copies, waits for them, and re-layouts: 216 us -> 151 us
  waiting for transfers between devices: 81.1 us -> 105 us
  blocking collectives: 57.3 us -> 44.2 us
    unnamed x28 -> x41, local copies, waits for them, and re-layouts: 156 us -> 109 us
    all_to_all x1 -> x0, local copies, waits for them, and re-layouts: 19.2 us -> none  [local(): lax.all_to_all(down_left, 'pop', split_axis=2, concat_axis=0, tiled=True)]
    all_to_all x1 -> x0, blocking collectives: 12.9 us -> none  [local(): lax.all_to_all(down_left, 'pop', split_axis=2, concat_axis=0, tiled=True)]
    all_gather x1, waiting for transfers between devices: 0.02 us -> 12.7 us  [local(): every_hidden = lax.all_gather(hidden, 'hid', axis=0, tiled=True)]
    reduce_scatter x1, waiting for transfers between devices: 33.9 us -> 45 us  [local(): lax.psum_scatter((jnp.dot(picked, down_weight, preferred_element_type=sca...]
    all_to_all x0 -> x1, starting transfers between devices: none -> 5.97 us  [local(): lax.all_to_all(jnp.stack(jnp.split(down_left, lax.axis_size('pop'), axis=...]
  transfers between devices with their start and end apart: 6 -> 7, of which waited for: 2 -> 3; matrix products, arithmetic and copies ran while one was open for 55% -> 46% of each run, Pallas kernels for 0% -> 0%
where the time goes in v1:
time: 372 us; the launch traced here: 370 us
  local copies, waits for them, and re-layouts  151 us (41%)
  waiting for transfers between devices  105 us (28%)
  blocking collectives  44.2 us (12%)
  matrix products  37.9 us (10%)
  between operations  14 us (4%)
  starting transfers between devices  13.4 us (4%)
  other arithmetic  4.88 us (1%)
    unnamed x41, local copies, waits for them, and re-layouts  109 us
    all_gather x1, waiting for transfers between devices, local(): gathered = lax.all_gather(tokens, 'pop', axis=0, tiled=True)  46.4 us
    reduce_scatter x1, waiting for transfers between devices, local(): lax.psum_scatter((jnp.dot(picked, down_weight, preferred_element_type=sca...  45 us
    all_gather x1, blocking collectives, local(): lax.all_gather(gate_projection, 'pop', axis=0, tiled=True)  21.7 us
    all_to_all x1, local copies, waits for them, and re-layouts, local(): lax.all_to_all(gate_output_factor, 'pop', split_axis=2, concat_axis=0, ti...  19.2 us
    all_to_all x1, local copies, waits for them, and re-layouts, local(): lax.all_to_all(up_output_factor, 'pop', split_axis=2, concat_axis=0, tile...  19.2 us
    all_gather x1, blocking collectives, local(): lax.all_gather(up_projection, 'pop', axis=0, tiled=True)  17.5 us
    all_gather x1, waiting for transfers between devices, local(): every_hidden = lax.all_gather(hidden, 'hid', axis=0, tiled=True)  12.7 us
  transfers between devices with their start and end apart: 7, of which 3 were waited for; matrix products, arithmetic and copies ran while one was open for 46% of the time, Pallas kernels for 0%

profile of v1, /device:TPU:0, one launch (start us, length us, event | category | flops | bytes accessed | tf_op | source)
XLA Modules:
  0.0 370.2 jit_solution(18268467448176289488)
XLA Ops:
  8.0 46.4 %all-gather.3.cloned.1.call-done = bf16[512,2048]{1,0:T(8,128)(2,1)} async-done(((bf16[32,2048]{1,0:T(8,128)(2,1)}), bf16[512,2048]{1,0:T(8,128)(2,1)}) %all-gather.3.cloned.1.call-update) | async-done | bytes 2097168 | tf_op jit(solution)/shard_map/all_gather | solution.py:68
  54.3 10.0 %fusion.8 = bf16[512,2048]{0,1:T(8,128)(2,1)} fusion(bf16[512,2048]{1,0:T(8,128)(2,1)} %all-gather.3.cloned.1.call-done, bf16[2048,1024]{1,0:T(8,128)(2,1)} %param.14, bf16[2048,1024]{1,0:T(8,128)(2,1)} %param.13), kind=kOutput, calls=%fused_computation.11 | convolution fusion | flops 4312793088 | bytes 12582912 | tf_op jit(solution)/shard_map/dot_general | solution.py:72
  64.3 13.0 %copy.24 = bf16[2,4,16384]{1,0,2:T(2,128)(2,1)} copy(bf16[2,4,16384]{2,1,0:T(4,128)(2,1)S(1)} %copy-done.6) | data formatting | bytes 524288 | tf_op args[8]
  77.3 16.9 %reshape.54 = bf16[16,2,4096]{2,1,0:T(2,128)(2,1)} reshape(bf16[16384,2,4]{2,1,0:T(2,128)(2,1)} %bitcast.75) | data formatting | bytes 524288
  94.2 3.5 all-to-all-start
  102.6 0.9 convolution_bitcast_fusion
  103.5 0.9 convolution_bitcast_fusion.1
  105.0 12.9 %copy.27 = bf16[2,4,16384]{1,0,2:T(2,128)(2,1)} copy(bf16[2,4,16384]{2,1,0:T(4,128)(2,1)S(1)} %copy-done.7) | data formatting | bytes 524288 | tf_op args[9]
  117.9 16.8 %reshape.52 = bf16[16,2,4096]{2,1,0:T(2,128)(2,1)} reshape(bf16[16384,2,4]{2,1,0:T(2,128)(2,1)} %bitcast.76) | data formatting | bytes 524288
  134.8 5.0 %all-reduce = (bf16[2,16,4]{1,2,0:T(4,128)(2,1)S(1)}, bf16[2,16,4]{1,2,0:T(4,128)(2,1)S(1)}) all-reduce(f32[2,16,4]{1,2,0:T(4,128)S(1)} %convolution_bitcast_fusion, f32[2,16,4]{1,2,0:T(4,128)S(1)} %convolution_bitcast_fusion.1), channel_id=1, replica_groups=mesh['pop'=16,'hid'=2] {'hid'}, use_global_device_ids=true, to_apply=%region_2.0 | all-reduce | flops 256 | bytes 1536 | tf_op jit(solution)/shard_map/psum | solution.py:53
  139.7 21.7 %all_gather.13 = bf16[32,16,4]{1,2,0:T(4,128)(2,1)S(1)} all-gather(bf16[2,16,4]{1,2,0:T(4,128)(2,1)S(1)} %get-tuple-element.5), channel_id=1, replica_groups=mesh['pop'=16,'hid'=2] {'pop'}, dimensions={0}, use_global_device_ids=true | all-gather | bytes 4352 | tf_op jit(solution)/shard_map/all_gather | solution.py:55
  161.4 17.5 %all_gather.14 = bf16[32,16,4]{1,2,0:T(4,128)(2,1)S(1)} all-gather(bf16[2,16,4]{1,2,0:T(4,128)(2,1)S(1)} %get-tuple-element.4), channel_id=1, replica_groups=mesh['pop'=16,'hid'=2] {'pop'}, dimensions={0}, use_global_device_ids=true | all-gather | bytes 4352 | tf_op jit(solution)/shard_map/all_gather | solution.py:56
  180.2 3.5 all-to-all-start.1
  185.1 19.0 %reshape.55 = bf16[16384,2,4]{2,1,0:T(2,128)(2,1)} reshape(bf16[16,2,4096]{2,1,0:T(2,128)(2,1)S(1)} %all-to-all-done) | data formatting | bytes 524288
  204.2 19.2 %copy.25 = bf16[2,4,16,1024]{3,1,0,2:T(4,128)(2,1)S(1)} copy(bf16[2,4,16,1024]{1,0,3,2:T(2,128)(2,1)} %bitcast.73) | data formatting | bytes 524288 | tf_op jit(solution)/shard_map/all_to_all | solution.py:59
  224.1 19.1 %reshape.53 = bf16[16384,2,4]{2,1,0:T(2,128)(2,1)} reshape(bf16[16,2,4096]{2,1,0:T(2,128)(2,1)S(1)} %all-to-all-done.1) | data formatting | bytes 524288
  243.2 19.2 %copy.28 = bf16[2,4,16,1024]{3,1,0,2:T(4,128)(2,1)S(1)} copy(bf16[2,4,16,1024]{1,0,3,2:T(2,128)(2,1)} %bitcast.74) | data formatting | bytes 524288 | tf_op jit(solution)/shard_map/all_to_all | solution.py:60
  263.4 1.4 convert_element_type.41
  264.8 1.2 fusion.14
  266.0 1.3 constant_dynamic-update-slice_fusion.2
  267.4 1.3 constant_dynamic-update-slice_fusion.1
  268.7 1.3 constant_dynamic-update-slice_fusion
  270.0 6.0 %all-to-all-start.2 = ((bf16[16,2,4,1024]{3,2,1,0:T(4,128)(2,1)}), bf16[16,2,4,1024]{3,2,1,0:T(4,128)(2,1)S(1)}, u32[]{:S(2)}, u32[]{:S(2)}) async-start(bf16[16,2,4,1024]{3,2,1,0:T(4,128)(2,1)} %constant_dynamic-update-slice_fusion), calls=%async_computation.3 | async-start | bytes 524288 | tf_op jit(solution)/shard_map/all_to_all | solution.py:62
  276.0 12.7 %all-gather.5.cloned.1.call-done = bf16[512,1024]{0,1:T(8,128)(2,1)} async-done(((bf16[256,1024]{0,1:T(8,128)(2,1)}), bf16[512,1024]{0,1:T(8,128)(2,1)}) %all-gather.5.cloned.1.call-update) | async-done | bytes 1048592 | tf_op jit(solution)/shard_map/all_gather | solution.py:97
  288.7 1.6 copy.30
  290.3 4.1 %convolution_multiply_fusion.3 = f32[32,16,2048]{2,1,0:T(8,128)} fusion(bf16[32,4,2048]{2,1,0:T(4,128)(2,1)} %param.18, bf16[32,16,1024]{2,1,0:T(8,128)(2,1)S(1)} %bitcast.79, bf16[32,4,1024]{2,1,0:T(4,128)(2,1)S(1)} %bitcast.80), kind=kOutput, calls=%fused_computation.9 | convolution fusion | flops 13631488 | bytes 6029312 | tf_op jit(solution)/shard_map/okw,owt->okt/dot_general | solution.py:107
  294.5 7.2 %fusion.4 = bf16[512,2048]{1,0:T(8,128)(2,1)} fusion(f32[32,16,2048]{2,1,0:T(8,128)} %convolution_multiply_fusion.3, bf16[512,1024]{0,1:T(8,128)(2,1)S(1)} %copy-done, bf16[1024,2048]{1,0:T(8,128)(2,1)} %param.15), kind=kOutput, calls=%fused_computation.8 | convolution fusion | flops 2149580800 | bytes 11534336 | tf_op jit(solution)/shard_map/dot_general | solution.py:112
  301.8 2.3 multiply_convert_fusion
  304.7 4.7 %convolution_multiply_fusion.1 = f32[2048,1024]{1,0:T(8,128)} fusion(bf16[128,2048]{1,0:T(8,128)(2,1)S(1)} %reshape.49, bf16[128,1024]{1,0:T(8,128)(2,1)S(1)} %reshape.50), kind=kOutput, calls=%fused_computation.5 | convolution fusion | flops 538968064 | bytes 9175040 | tf_op jit(solution)/shard_map/dot_general | solution.py:143
  309.3 4.7 %convolution_multiply_fusion.2 = f32[2048,1024]{1,0:T(8,128)} fusion(bf16[128,2048]{1,0:T(8,128)(2,1)S(1)} %reshape.47, bf16[128,1024]{1,0:T(8,128)(2,1)S(1)} %reshape.48), kind=kOutput, calls=%fused_computation.6 | convolution fusion | flops 538968064 | bytes 9175040 | tf_op jit(solution)/shard_map/dot_general | solution.py:137
  314.0 4.7 %convolution_multiply_fusion = f32[1024,2048]{1,0:T(8,128)} fusion(bf16[128,1024]{1,0:T(8,128)(2,1)S(1)} %reshape_reshape.3, bf16[128,2048]{1,0:T(8,128)(2,1)S(1)} %reshape.51), kind=kOutput, calls=%fused_computation.4 | convolution fusion | flops 538968064 | bytes 9175040 | tf_op jit(solution)/shard_map/dot_general | solution.py:149
  318.7 45.0 %reduce-scatter.5.cloned.1.call-done = bf16[32,2048]{1,0:T(8,128)(2,1)} async-done(((bf16[512,2048]{1,0:T(8,128)(2,1)}), bf16[32,2048]{1,0:T(8,128)(2,1)}) %reduce-scatter.5.cloned.1.call-update) | async-done | bytes 131088 | tf_op jit(solution)/shard_map/reduce_scatter | solution.py:110
  (56 shorter events, 11.3 us)
Async XLA Ops:
  7.2 47.2 %all-gather.3.cloned.1.call-start = ((), (), s32[]{:S(2)}) async-start(), calls=%async_computation.5 | async-start | bytes 2228224 | tf_op jit(solution)/shard_map/all_gather | solution.py:68
  7.9 56.4 %copy-start.6 = (bf16[2,4,16384]{2,1,0:T(4,128)(2,1)S(1)}, bf16[2,4,16384]{2,1,0:T(4,128)(2,1)}, u32[]{:S(2)}) copy-start(bf16[2,4,16384]{2,1,0:T(4,128)(2,1)} %param.19) | copy-start | bytes 786436
  7.9 255.5 %reduce-scatter.3.cloned.1.call-start = ((), (), s32[]{:S(2)}) async-start(), calls=%async_computation.6 | async-start | bytes 3145728 | tf_op jit(solution)/shard_map/reduce_scatter | solution.py:71
  77.3 20.4 %copy-start.8 = (bf16[2,4,16384]{2,1,0:T(4,128)(2,1)S(1)}, bf16[2,4,16384]{2,1,0:T(4,128)(2,1)}, u32[]{:S(2)}) copy-start(bf16[2,4,16384]{2,1,0:T(4,128)(2,1)} %param.21) | copy-start | bytes 786436
  77.3 25.3 %copy-start.4 = (bf16[32,2048]{1,0:T(8,128)(2,1)S(1)}, bf16[32,2048]{1,0:T(8,128)(2,1)}, u32[]{:S(2)}) copy-start(bf16[32,2048]{1,0:T(8,128)(2,1)} %param.11) | copy-start | bytes 393220
  77.3 27.7 %copy-start.7 = (bf16[2,4,16384]{2,1,0:T(4,128)(2,1)S(1)}, bf16[2,4,16384]{2,1,0:T(4,128)(2,1)}, u32[]{:S(2)}) copy-start(bf16[2,4,16384]{2,1,0:T(4,128)(2,1)} %param.20) | copy-start | bytes 786436
  94.2 86.0 %all-to-all-start = ((bf16[16,2,4096]{2,1,0:T(2,128)(2,1)}), bf16[16,2,4096]{2,1,0:T(2,128)(2,1)S(1)}, u32[]{:S(2)}, u32[]{:S(2)}) async-start(bf16[16,2,4096]{2,1,0:T(2,128)(2,1)} %reshape.54), calls=%async_computation.1 | async-start | bytes 524288 | tf_op jit(solution)/shard_map/all_to_all | solution.py:59
  180.2 43.9 %all-to-all-start.1 = ((bf16[16,2,4096]{2,1,0:T(2,128)(2,1)}), bf16[16,2,4096]{2,1,0:T(2,128)(2,1)S(1)}, u32[]{:S(2)}, u32[]{:S(2)}) async-start(bf16[16,2,4096]{2,1,0:T(2,128)(2,1)} %reshape.52), calls=%async_computation.2 | async-start | bytes 524288 | tf_op jit(solution)/shard_map/all_to_all | solution.py:60
  183.7 105.0 %all-gather.5.cloned.1.call-start = ((), (), s32[]{:S(2)}) async-start(), calls=%async_computation.7 | async-start | bytes 1572864 | tf_op jit(solution)/shard_map/all_gather | solution.py:97
  262.3 0.7 copy-start.2
  270.0 20.3 %all-to-all-start.2 = ((bf16[16,2,4,1024]{3,2,1,0:T(4,128)(2,1)}), bf16[16,2,4,1024]{3,2,1,0:T(4,128)(2,1)S(1)}, u32[]{:S(2)}, u32[]{:S(2)}) async-start(bf16[16,2,4,1024]{3,2,1,0:T(4,128)(2,1)} %constant_dynamic-update-slice_fusion), calls=%async_computation.3 | async-start | bytes 524288 | tf_op jit(solution)/shard_map/all_to_all | solution.py:62
  276.0 87.7 %reduce-scatter.5.cloned.1.call-start = ((), (), s32[]{:S(2)}) async-start(), calls=%async_computation.8 | async-start | bytes 2228224 | tf_op jit(solution)/shard_map/reduce_scatter | solution.py:110
  288.7 5.7 %copy-start = (bf16[512,1024]{0,1:T(8,128)(2,1)S(1)}, bf16[512,1024]{0,1:T(8,128)(2,1)}, u32[]{:S(2)}) copy-start(bf16[512,1024]{0,1:T(8,128)(2,1)} %all-gather.5.cloned.1.call-done) | copy-start | bytes 3145732
  294.4 7.3 %copy-start.9 = (s32[32]{0:T(128)S(1)}, s32[32]{0:T(128)}, u32[]{:S(2)}) copy-start(s32[32]{0:T(128)} %param.12) | copy-start | bytes 388
  294.4 7.3 %copy-start.1 = (bf16[32,4,2048]{2,1,0:T(4,128)(2,1)S(1)}, bf16[32,4,2048]{2,1,0:T(4,128)(2,1)}, u32[]{:S(2)}) copy-start(bf16[32,4,2048]{2,1,0:T(4,128)(2,1)} %param.18) | copy-start | bytes 1572868
  294.4 7.3 %copy-start.5 = (bf16[32,4,2048]{2,1,0:T(4,128)(2,1)S(1)}, bf16[32,4,2048]{2,1,0:T(4,128)(2,1)}, u32[]{:S(2)}) copy-start(bf16[32,4,2048]{2,1,0:T(4,128)(2,1)} %param.17) | copy-start | bytes 1572868
  301.7 2.7 copy-start.3
Sparse Core Ops, SparseCore 0:
  10.1 44.1 all-gather.2
  64.5 30.6 reduce-scatter.2
  266.2 22.5 all-gather.4
  301.9 61.7 reduce-scatter.4
